TPU v7x, 32 devices: a whole 2x2x4 slice. The times are simulated.
32 devices in a mesh: groups: 2 (over y), ctx: 4 (over z), ep: 2 (over x), tp: 2 (over core).
Axes of the slice: x: 2, y: 2, z: 4, core: 2. Of those that a mesh axis runs over, the one named last changes fastest.
Arguments:
- queries: bfloat16 [4, 512, 5120], P(('groups', 'ep'), 'ctx', 'tp'), parts along dimension 0, may hold values from -128 to 128
- keys: bfloat16 [4, 512, 1024], P(('groups', 'ep'), 'ctx', 'tp'), parts along dimension 0, may hold values from -6 to 6
- values: bfloat16 [4, 512, 1024], P(('groups', 'ep'), 'ctx', 'tp'), parts along dimension 0, may hold values from -6 to 6
- expert_ids: int32 [4, 512, 1], P(('groups', 'ep'), 'ctx'), parts along dimension 0, may hold values from 0 to 127, as said below
- router: bfloat16 [5120, 2], P('tp', 'ep'), may hold values from -0.3125 to 0.3125
- w_gate: bfloat16 [2, 5120, 4096], P('ep', 'tp', 'ctx'), may hold values from -0.3125 to 0.3125
- w_up: bfloat16 [2, 5120, 4096], P('ep', 'tp', 'ctx'), may hold values from -0.3125 to 0.3125
- w_down: bfloat16 [2, 4096, 5120], P('ep', 'ctx', 'tp'), may hold values from -0.09375 to 0.09375
Outputs:
- layer_out: bfloat16 [4, 512, 5120], P(('groups', 'ep'), 'ctx', 'tp'), parts along dimension 0
There are 2 independent parts, one for each index of `groups`. A program takes and returns all parts, laid end to end along the dimension named above; an argument that names none is the same for every part. Nothing has to cross between parts.
Inputs may be any that keep to these rules, and one draw needn't show every extreme that they name: `expert_ids`: among the positions of one device, each expert below 2 is named at most 2 times; in every draw one of them is named exactly 2 times on every device.
All inputs are finite; a program needn't handle non-finite values.
Results may differ from a plain program's by a relative error of at most 0.023.
Values may be sent and summed in bfloat16 or wider, within the bound.
A program may use at most 64 MiB of HBM per device.

v0:
```python
import jax
import jax.numpy as jnp
from jax import lax
from jax.sharding import PartitionSpec as P

HEAD_WIDTH = 128
CAP = 2


def block_width(key_count):
    for candidate in (512, 256, 128):
        return candidate
    return key_count


def fresh_state(query_rows, kv_heads, group_width):
    return (
        jnp.full((kv_heads, group_width, query_rows), -1e30, jnp.float32),
        jnp.zeros((kv_heads, group_width, query_rows), jnp.float32),
        jnp.zeros((query_rows, kv_heads, group_width, HEAD_WIDTH), jnp.float32),
    )


def absorb_block(status, query_half, query_pos, key_block, value_block, key_pos):
    old_max, totals, weighted = status
    scores = jnp.einsum(
        "rgqd,kgd->gqrk", query_half, key_block, preferred_element_type=jnp.float32
    ) * HEAD_WIDTH ** (-0.5)
    visible = query_pos[:, None] >= key_pos[None, :]
    scores = jnp.where(visible, scores, -1e30)
    running_max = jnp.maximum(old_max, jnp.max(scores, axis=3))
    factor = jnp.exp(old_max - running_max)
    weights = jnp.where(visible, jnp.exp(scores - running_max[..., None]), 0.0)
    totals = totals * factor + jnp.sum(weights, axis=3)
    update = jnp.einsum(
        "gqrk,kgd->rgqd",
        weights.astype(jnp.bfloat16),
        value_block,
        preferred_element_type=jnp.float32,
    )
    weighted = weighted * jnp.transpose(factor, (2, 0, 1))[..., None] + update
    return (running_max, totals, weighted)


def finish(status, row_count):
    old_max, totals, weighted = status
    normed = weighted / jnp.transpose(totals, (2, 0, 1))[..., None]
    return normed.astype(jnp.bfloat16).reshape(row_count, -1)


def shards(queries, keys, values, expert_ids, router, w_gate, w_up, w_down):
    row_count = queries.shape[1]
    half_rows = row_count // 2
    feature_width = queries.shape[2]
    kv_heads = keys.shape[2] // HEAD_WIDTH
    group_width = feature_width // HEAD_WIDTH // kv_heads
    ep_count = lax.axis_size("ep")
    ctx_place = lax.axis_index("ctx")
    local_queries = queries[0].reshape(row_count, kv_heads, group_width, HEAD_WIDTH)
    lead_half = local_queries[:half_rows]
    tail_half = local_queries[half_rows:]
    lead_pos = ctx_place * row_count + jnp.arange(half_rows, dtype=jnp.int32)
    tail_pos = ctx_place * row_count + half_rows + jnp.arange(half_rows, dtype=jnp.int32)
    initial = (
        fresh_state(half_rows, kv_heads, group_width),
        fresh_state(half_rows, kv_heads, group_width),
    )
    key_piece = lax.all_gather(keys, "ctx", axis=1, tiled=True)[0]
    key_count = key_piece.shape[0]
    key_block_rows = block_width(key_count)
    block_count = key_count // key_block_rows
    key_blocks = key_piece.reshape(block_count, key_block_rows, kv_heads, HEAD_WIDTH)
    value_blocks = lax.all_gather(values, "ctx", axis=1, tiled=True)[0].reshape(
        block_count, key_block_rows, kv_heads, HEAD_WIDTH
    )
    offsets = jnp.arange(block_count, dtype=jnp.int32) * key_block_rows

    def one_block(status, inputs):
        key_block, value_block, block_begin = inputs
        key_pos = block_begin + jnp.arange(key_block_rows, dtype=jnp.int32)
        lead_state = lax.cond(
            block_begin <= lead_pos[-1],
            lambda kept_state: absorb_block(
                kept_state, lead_half, lead_pos, key_block, value_block, key_pos
            ),
            lambda kept_state: kept_state,
            status[0],
        )
        tail_state = lax.cond(
            block_begin <= tail_pos[-1],
            lambda kept_state: absorb_block(
                kept_state, tail_half, tail_pos, key_block, value_block, key_pos
            ),
            lambda kept_state: kept_state,
            status[1],
        )
        return ((lead_state, tail_state), None)

    result, _ = lax.scan(one_block, initial, (key_blocks, value_blocks, offsets))
    lead_status, tail_status = result
    lead_out = finish(lead_status, half_rows)
    tail_out = finish(tail_status, half_rows)
    attended = jnp.concatenate([lead_out, tail_out], axis=0)
    chosen = expert_ids[0, :, 0]
    choose = (chosen[:, None] == jnp.arange(ep_count, dtype=jnp.int32)[None, :]).astype(jnp.int32)
    earlier = jnp.cumsum(choose, axis=0) - choose
    slot_index = jnp.sum(earlier * choose, axis=1)
    target = chosen * CAP + slot_index
    spread = (target[None, :] == jnp.arange(ep_count * CAP, dtype=jnp.int32)[:, None]).astype(
        jnp.bfloat16
    )
    outgoing = jnp.dot(spread, attended, preferred_element_type=jnp.float32).astype(jnp.bfloat16)
    arrived = lax.all_to_all(
        outgoing.reshape(ep_count, CAP, feature_width),
        "ep",
        split_axis=0,
        concat_axis=0,
        tiled=True,
    )
    gathered = lax.all_gather(arrived[None], "ctx", axis=0, tiled=True)
    members = gathered.reshape(-1, feature_width)
    gate_w = w_gate[0]
    up_w = w_up[0]
    down_w = w_down[0]
    gate_part = jnp.dot(members, gate_w, preferred_element_type=jnp.float32)
    up_part = jnp.dot(members, up_w, preferred_element_type=jnp.float32)
    score_part = jnp.dot(members, router, preferred_element_type=jnp.float32)
    gate_sum, up_sum, router_score = (
        lax.psum(gate_part.astype(jnp.bfloat16), "tp").astype(jnp.float32),
        lax.psum(up_part.astype(jnp.bfloat16), "tp").astype(jnp.float32),
        lax.psum(score_part.astype(jnp.bfloat16), "tp").astype(jnp.float32),
    )
    weight = jax.nn.sigmoid(router_score)
    hidden = (jax.nn.silu(weight * gate_sum) * (weight * up_sum)).astype(jnp.bfloat16)
    expert_rows = lax.psum_scatter(
        jnp.dot(hidden, down_w, preferred_element_type=jnp.float32).astype(jnp.bfloat16),
        "ctx",
        scatter_dimension=0,
        tiled=True,
    )
    returned = lax.all_to_all(
        expert_rows.reshape(ep_count, CAP, feature_width),
        "ep",
        split_axis=0,
        concat_axis=0,
        tiled=True,
    )
    returned = returned.reshape(ep_count * CAP, feature_width)
    routed = lax.dot_general(
        spread, returned, (((0,), (0,)), ((), ())), preferred_element_type=jnp.float32
    )
    layer_out = (attended.astype(jnp.float32) + routed).astype(jnp.bfloat16)
    return layer_out[None]


def solution(mesh):
    placed = (
        P(("groups", "ep"), "ctx", "tp"),
        P(("groups", "ep"), "ctx", "tp"),
        P(("groups", "ep"), "ctx", "tp"),
        P(("groups", "ep"), "ctx", None),
        P("tp", "ep"),
        P("ep", "tp", "ctx"),
        P("ep", "tp", "ctx"),
        P("ep", "ctx", "tp"),
    )
    return jax.shard_map(
        shards,
        mesh=mesh,
        in_specs=placed,
        out_specs=P(("groups", "ep"), "ctx", "tp"),
        check_vma=False,
    )
```

profile of v0, /device:TPU:0, one launch (start us, length us, event | category | flops | bytes accessed | tf_op | source)
XLA Modules:
  0.0 157.5 jit_solution(6667889364840034550)
XLA Ops:
  6.5 0.0 copy-start
  6.5 0.0 all-reduce.7.cloned.1.call-start
  6.5 1.0 copy.23
  7.6 16.7 %all_gather.9 = bf16[1,512,512]{1,2,0:T(8,128)(2,1)S(1)} all-gather(bf16[1,128,512]{1,2,0:T(8,128)(2,1)S(1)} %copy.23), channel_id=1, replica_groups=mesh['groups'=2,'ctx'=4,'ep'=2,'tp'=2] {'ctx'}, dimensions={1}, use_global_device_ids=true | all-gather | bytes 655360 | tf_op jit(solution)/shard_map/all_gather | solution.py:68
  24.3 1.0 copy.24
  25.3 14.6 %all_gather.10 = bf16[1,512,512]{1,2,0:T(8,128)(2,1)S(1)} all-gather(bf16[1,128,512]{1,2,0:T(8,128)(2,1)S(1)} %copy.24), channel_id=1, replica_groups=mesh['groups'=2,'ctx'=4,'ep'=2,'tp'=2] {'ctx'}, dimensions={1}, use_global_device_ids=true | all-gather | bytes 655360 | tf_op jit(solution)/shard_map/all_gather | solution.py:73
  39.9 0.6 slice.23
  41.1 0.1 broadcast.44
  41.2 0.6 broadcast.43
  41.8 4.8 %conditional.3 = (f32[4,5,64]{2,1,0:T(8,128)S(1)}, f32[64,4,5,128]{3,0,2,1:T(8,128)S(1)}) conditional(s32[]{:T(128)} %bitcast.14, (f32[4,5,64]{2,1,0:T(8,128)}, f32[64,4,5,128]{3,0,2,1:T(8,128)S(1)}) %tuple.31, (s32[64]{0:T(128)S(1)}, s32[512]{0:T(512)S(1)}, bf16[1,128,2560]{2,1,0:T(8,128)(2,1)}, bf16[512,4,128]{0,2,1:T(8,128)(2,1)S(1)}, ...), branch_computations={%region_4.5_spmd, %region_5.0_spmd} | conditional | flops 344428288 | bytes 12067088 | solution.py:89
  41.8 0.1 broadcast_compare_fusion.1
  41.9 1.0 slice.18
  42.9 0.4 slice.19
  43.3 0.7 fusion.20
  44.0 0.9 fusion.22
  44.9 0.7 multiply_add_fusion.1
  45.6 1.1 fusion.29
  46.7 0.0 copy-start.1
  46.7 0.2 divide_convert_fusion
  46.9 0.2 copy.30
  47.2 0.4 reshape.57
  47.6 0.6 slice.22
  48.8 0.0 copy-done.1
  48.8 5.9 %conditional.2 = ((f32[4,5,64]{2,1,0:T(8,128)}, f32[64,4,5,128]{3,0,2,1:T(8,128)S(1)})) conditional(s32[]{:T(128)} %bitcast.10, (f32[4,5,64]{2,1,0:T(8,128)}, f32[64,4,5,128]{3,0,2,1:T(8,128)S(1)}) %tuple.31, (s32[64]{0:T(128)S(1)}, s32[512]{0:T(512)S(1)}, bf16[1,128,2560]{2,1,0:T(8,128)(2,1)S(1)}, bf16[512,4,128]{0,2,1:T(8,128)(2,1)S(1)}, ...), branch_computations={%region_0.1_spmd, %region_1.4_spmd} | conditional | flops 344428288 | bytes 12239212 | solution.py:81
  48.8 0.0 copy-start.2
  48.8 0.7 broadcast_compare_fusion
  49.5 0.0 copy-done.2
  49.6 0.0 copy-start.3
  49.6 0.0 copy-start.4
  49.6 0.4 slice.17
  50.0 1.4 fusion
  51.4 0.0 copy-done.3
  51.4 0.0 copy-done.4
  51.4 0.9 fusion.2
  52.3 1.3 multiply_add_fusion
  53.6 1.1 fusion.9
  54.7 0.0 copy-start.5
  54.7 1.0 divide_convert_fusion.1
  55.7 0.2 copy.27
  55.9 0.4 reshape.56
  56.3 0.0 copy-done.5
  56.4 0.1 fusion.59
  56.4 0.2 reduce_window_sum.11
  56.6 0.2 select_reduce_fusion
  56.8 0.2 convolution_convert_fusion
  57.1 6.4 %all_to_all.10 = bf16[2,2,2560]{2,1,0:T(2,128)(2,1)S(1)} all-to-all(bf16[2,2,2560]{2,1,0:T(2,128)(2,1)S(1)} %reshape.58), channel_id=1, replica_groups=mesh['groups'=2,'ctx'=4,'ep'=2,'tp'=2] {'ep'}, dimensions={0} | all-to-all | bytes 40960 | tf_op jit(solution)/shard_map/all_to_all | solution.py:113
  63.5 13.2 %all-gather = bf16[8,2,2560]{2,1,0:T(2,128)(2,1)S(1)} all-gather(bf16[2,2,2560]{2,1,0:T(2,128)(2,1)S(1)} %all_to_all.10), channel_id=2, replica_groups=mesh['groups'=2,'ctx'=4,'ep'=2,'tp'=2] {'ctx'}, dimensions={0}, use_global_device_ids=true | all-gather | bytes 102400 | tf_op jit(solution)/shard_map/all_gather | solution.py:120
  76.7 3.9 %fusion.51 = bf16[16,1024]{1,0:T(8,128)(2,1)} fusion(bf16[16,2560]{1,0:T(8,128)(2,1)S(1)} %reshape.59, bf16[1,2560,1024]{2,1,0:T(8,128)(2,1)} %param.17), kind=kOutput, calls=%fused_computation.51 | convolution fusion | flops 83902464 | bytes 5357568 | tf_op jit(solution)/shard_map/dot_general | solution.py:125
  80.6 3.9 %fusion.54 = bf16[16,1024]{1,0:T(8,128)(2,1)} fusion(bf16[16,2560]{1,0:T(8,128)(2,1)S(1)} %reshape.59, bf16[1,2560,1024]{2,1,0:T(8,128)(2,1)} %param.18), kind=kOutput, calls=%fused_computation.52 | convolution fusion | flops 83902464 | bytes 5357568 | tf_op jit(solution)/shard_map/dot_general | solution.py:126
  84.6 0.0 copy-done
  84.6 0.6 fusion.58
  85.2 0.0 all-reduce.7.cloned.1.call-update
  85.2 0.0 all-reduce.5.cloned.1.call-start
  85.3 16.5 %all-reduce.7.cloned.1.call-done = (bf16[16,1024]{1,0:T(8,128)(2,1)}, bf16[16,1024]{1,0:T(8,128)(2,1)}, bf16[16,1]{0,1:T(2,128)(2,1)}) async-done(((bf16[16,1024]{1,0:T(8,128)(2,1)}, bf16[16,1024]{1,0:T(8,128)(2,1)}, bf16[16,1]{0,1:T(2,128)(2,1)}), (bf16[16,1024]{1,0:T(8,128)(2,1)}, bf16[16,1024]{1,0:T(8,128)(2,1)}, bf16[16,1]{0,1:T(2,128)(2,1)})) %all-reduce.7.cloned.1.call-update) | async-done | bytes 65584 | tf_op jit(solution)/shard_map/psum | solution.py:130
  101.8 0.7 divide_bitcast_fusion
  102.5 0.0 copy-start.6
  102.5 4.0 %fusion.48 = bf16[16,2560]{1,0:T(8,128)(2,1)} fusion(bf16[1,1024,2560]{2,1,0:T(8,128)(2,1)} %param.19, bf16[16,1024]{1,0:T(8,128)(2,1)} %get-tuple-element.178, bf16[16,1024]{1,0:T(8,128)(2,1)} %get-tuple-element.179, f32[16]{0:T(128)S(1)} %divide_bitcast_fusion), kind=kOutput, calls=%fused_computation.49 | convolution fusion | flops 84090880 | bytes 5390400 | tf_op jit(solution)/shard_map/dot_general | solution.py:136
  106.5 0.0 all-reduce.5.cloned.1.call-update
  106.6 0.0 copy-done.6
  106.6 0.6 dynamic-slice
  107.7 34.5 %all-reduce.5.cloned.1.call-done = bf16[16,2560]{1,0:T(8,128)(2,1)} async-done(((bf16[16,2560]{1,0:T(8,128)(2,1)}), bf16[16,2560]{1,0:T(8,128)(2,1)}) %all-reduce.5.cloned.1.call-update) | async-done | bytes 81936
  142.2 0.8 constant_dynamic-slice_fusion
  143.0 6.4 %all_to_all.11 = bf16[2,2,2560]{2,1,0:T(2,128)(2,1)S(1)} all-to-all(bf16[2,2,2560]{2,1,0:T(2,128)(2,1)S(1)} %reshape.61), channel_id=1, replica_groups=mesh['groups'=2,'ctx'=4,'ep'=2,'tp'=2] {'ep'}, dimensions={0} | all-to-all | bytes 40960 | tf_op jit(solution)/shard_map/all_to_all | solution.py:141
  149.5 1.2 fusion.47
  (15 shorter events, 0.2 us)
Async XLA Ops:
  6.5 78.0 %copy-start = (bf16[2560,1]{0,1:T(2,128)(2,1)S(1)}, bf16[2560,1]{0,1:T(2,128)(2,1)}, u32[]{:S(2)}) copy-start(bf16[2560,1]{0,1:T(2,128)(2,1)} %param.16) | copy-start | bytes 15364
  6.5 95.3 %all-reduce.7.cloned.1.call-start = ((), (), s32[]{:S(2)}) async-start(), calls=%async_computation.3 | async-start | bytes 132096 | tf_op jit(solution)/shard_map/psum | solution.py:130
  46.7 2.1 %copy-start.1 = (bf16[1,128,2560]{2,1,0:T(8,128)(2,1)S(1)}, bf16[1,128,2560]{2,1,0:T(8,128)(2,1)}, u32[]{:S(2)}) copy-start(bf16[1,128,2560]{2,1,0:T(8,128)(2,1)} %param.12) | copy-start | bytes 1966084
  48.8 0.7 copy-start.2
  49.6 1.8 %copy-start.3 = (f32[4,5,64]{2,1,0:T(8,128)S(1)}, f32[4,5,64]{2,1,0:T(8,128)}, u32[]{:S(2)}) copy-start(f32[4,5,64]{2,1,0:T(8,128)} %copy-done.2) | copy-start | bytes 15364 | tf_op jit(solution)/shard_map/while/body/eval_jaxpr/cond
  49.6 1.9 %copy-start.4 = (pred[64,512]{1,0:T(8,128)(4,1)S(1)}, pred[64,512]{1,0:T(8,128)(4,1)}, u32[]{:S(2)}) copy-start(pred[64,512]{1,0:T(8,128)(4,1)} %broadcast_compare_fusion) | copy-start | bytes 98308 | tf_op jit(solution)/shard_map/while/body/eval_jaxpr/cond
  54.7 1.6 %copy-start.5 = (s32[1,128,1]{1,2,0:T(1,128)S(1)}, s32[1,128,1]{1,2,0:T(1,128)}, u32[]{:S(2)}) copy-start(s32[1,128,1]{1,2,0:T(1,128)} %param.15) | copy-start | bytes 1540
  85.2 57.0 %all-reduce.5.cloned.1.call-start = ((), (), s32[]{:S(2)}) async-start(), calls=%async_computation.2 | async-start | bytes 163840
  102.5 4.1 %copy-start.6 = (u32[32]{0:T(128)S(1)}, u32[32]{0:T(128)}, u32[]{:S(2)}) copy-start(u32[32]{0:T(128)} %constant.73) | copy-start | bytes 388
Sparse Core Ops, SparseCore 0:
  85.3 16.4 all-reduce.6
  106.7 35.4 all-reduce.4
where the time goes:
time: 158 us
  blocking collectives  57.4 us (36%)
  waiting for transfers between devices  51.1 us (32%)
  matrix products  18.1 us (11%)
  between operations  15.5 us (10%)
  local copies, waits for them, and re-layouts  8.44 us (5%)
  other arithmetic  6.94 us (4%)
    unnamed x3, waiting for transfers between devices  34.5 us
    all_gather x1, blocking collectives, shards(): key_piece = lax.all_gather(keys, 'ctx', axis=1, tiled=True)[0]  16.7 us
    psum x1, waiting for transfers between devices, shards(): lax.psum(up_part.astype(jnp.bfloat16), 'tp').astype(jnp.float32)  16.5 us
    all_gather x1, blocking collectives, shards(): lax.all_gather(values, 'ctx', axis=1, tiled=True)[0]  14.6 us
    all_gather x1, blocking collectives, shards(): gathered = lax.all_gather(arrived[None], 'ctx', axis=0, tiled=True)  13.2 us
    all_to_all x1, blocking collectives, shards(): lax.all_to_all(outgoing.reshape(ep_count, CAP, feature_width), 'ep', spli...  6.44 us
    all_to_all x1, blocking collectives, shards(): lax.all_to_all(expert_rows.reshape(ep_count, CAP, feature_width), 'ep', s...  6.41 us
    dot_general x1, matrix products, shards(): jnp.dot(hidden, down_w, preferred_element_type=jnp.float32)  4.03 us
  transfers between devices with their start and end apart: 2, of which 2 were waited for; matrix products, arithmetic and copies ran while one was open for 0% of the time, Pallas kernels for 0%

commit v1 on v0

--- a/solution.py
+++ b/solution.py
@@ -125,9 +125,10 @@
     gate_part = jnp.dot(members, gate_w, preferred_element_type=jnp.float32)
     up_part = jnp.dot(members, up_w, preferred_element_type=jnp.float32)
     score_part = jnp.dot(members, router, preferred_element_type=jnp.float32)
+    entries_produce = lambda frame: jnp.sum(lax.all_gather(frame, "tp"), axis=0)
     gate_sum, up_sum, router_score = (
         lax.psum(gate_part.astype(jnp.bfloat16), "tp").astype(jnp.float32),
-        lax.psum(up_part.astype(jnp.bfloat16), "tp").astype(jnp.float32),
+        entries_produce(up_part.astype(jnp.bfloat16)).astype(jnp.float32),
         lax.psum(score_part.astype(jnp.bfloat16), "tp").astype(jnp.float32),
     )
     weight = jax.nn.sigmoid(router_score)

time: 158 us -> 142 us (0.90)
  waiting for transfers between devices: 51.1 us -> 31.7 us
  blocking collectives: 57.4 us -> 62.7 us
  matrix products: 18.1 us -> 16.3 us
    psum x1 -> x0, waiting for transfers between devices: 16.5 us -> none  [shards(): lax.psum(up_part.astype(jnp.bfloat16), 'tp').astype(jnp.float32)]
    psum x0 -> x1, blocking collectives: none -> 3.46 us  [shards(): lax.psum(gate_part.astype(jnp.bfloat16), 'tp').astype(jnp.float32)]
    unnamed x3 -> x2, waiting for transfers between devices: 34.5 us -> 31.7 us
    all_gather x0 -> x1, blocking collectives: none -> 1.85 us  [shards(): entries_produce = lambda frame: jnp.sum(lax.all_gather(frame, 'tp'), axis=0)]
  transfers between devices with their start and end apart: 2 -> 1, of which waited for: 2 -> 1; matrix products, arithmetic and copies ran while one was open for 0% -> 0% of each run, Pallas kernels for 0% -> 0%
where the time goes in v1:
time: 142 us; the launch traced here: 141 us
  blocking collectives  62.7 us (44%)
  waiting for transfers between devices  31.7 us (22%)
  matrix products  16.3 us (11%)
  between operations  15.5 us (11%)
  local copies, waits for them, and re-layouts  8.46 us (6%)
  other arithmetic  6.27 us (4%)
    unnamed x2, waiting for transfers between devices  31.7 us
    all_gather x1, blocking collectives, shards(): key_piece = lax.all_gather(keys, 'ctx', axis=1, tiled=True)[0]  16.7 us
    all_gather x1, blocking collectives, shards(): lax.all_gather(values, 'ctx', axis=1, tiled=True)[0]  14.6 us
    all_gather x1, blocking collectives, shards(): gathered = lax.all_gather(arrived[None], 'ctx', axis=0, tiled=True)  13.2 us
    all_to_all x1, blocking collectives, shards(): lax.all_to_all(outgoing.reshape(ep_count, CAP, feature_width), 'ep', spli...  6.44 us
    all_to_all x1, blocking collectives, shards(): lax.all_to_all(expert_rows.reshape(ep_count, CAP, feature_width), 'ep', s...  6.42 us
    dot_general x1, matrix products, shards(): jnp.dot(hidden, down_w, preferred_element_type=jnp.float32)  3.98 us
    unnamed x13, local copies, waits for them, and re-layouts  3.47 us
  transfers between devices with their start and end apart: 1, of which 1 were waited for; matrix products, arithmetic and copies ran while one was open for 0% of the time, Pallas kernels for 0%

profile of v1, /device:TPU:0, one launch (start us, length us, event | category | flops | bytes accessed | tf_op | source)
XLA Modules:
  0.0 141.0 jit_solution(17248721225384586135)
XLA Ops:
  6.5 0.0 copy-start
  6.5 0.0 all-reduce.4.cloned.1.call-start
  6.5 1.0 copy.23
  7.6 16.7 %all_gather.15 = bf16[1,512,512]{1,2,0:T(8,128)(2,1)S(1)} all-gather(bf16[1,128,512]{1,2,0:T(8,128)(2,1)S(1)} %copy.23), channel_id=1, replica_groups=mesh['groups'=2,'ctx'=4,'ep'=2,'tp'=2] {'ctx'}, dimensions={1}, use_global_device_ids=true | all-gather | bytes 655360 | tf_op jit(solution)/shard_map/all_gather | solution.py:68
  24.3 1.0 copy.24
  25.3 14.6 %all_gather.16 = bf16[1,512,512]{1,2,0:T(8,128)(2,1)S(1)} all-gather(bf16[1,128,512]{1,2,0:T(8,128)(2,1)S(1)} %copy.24), channel_id=1, replica_groups=mesh['groups'=2,'ctx'=4,'ep'=2,'tp'=2] {'ctx'}, dimensions={1}, use_global_device_ids=true | all-gather | bytes 655360 | tf_op jit(solution)/shard_map/all_gather | solution.py:73
  39.9 0.6 slice.23
  41.1 0.1 broadcast.44
  41.2 0.6 broadcast.43
  41.8 4.8 %conditional.3 = (f32[4,5,64]{2,1,0:T(8,128)S(1)}, f32[64,4,5,128]{3,0,2,1:T(8,128)S(1)}) conditional(s32[]{:T(128)} %bitcast.14, (f32[4,5,64]{2,1,0:T(8,128)}, f32[64,4,5,128]{3,0,2,1:T(8,128)S(1)}) %tuple.31, (s32[64]{0:T(128)S(1)}, s32[512]{0:T(512)S(1)}, bf16[1,128,2560]{2,1,0:T(8,128)(2,1)}, bf16[512,4,128]{0,2,1:T(8,128)(2,1)S(1)}, ...), branch_computations={%region_4.5_spmd, %region_5.0_spmd} | conditional | flops 344428288 | bytes 12067088 | solution.py:89
  41.8 0.1 broadcast_compare_fusion.1
  41.9 1.0 slice.18
  42.9 0.4 slice.19
  43.3 0.7 fusion.20
  44.0 0.9 fusion.22
  44.9 0.7 multiply_add_fusion.1
  45.6 1.1 fusion.29
  46.7 0.0 copy-start.1
  46.7 0.2 divide_convert_fusion
  46.9 0.2 copy.30
  47.2 0.4 reshape.57
  47.5 0.6 slice.22
  48.8 0.0 copy-done.1
  48.8 5.9 %conditional.2 = ((f32[4,5,64]{2,1,0:T(8,128)}, f32[64,4,5,128]{3,0,2,1:T(8,128)S(1)})) conditional(s32[]{:T(128)} %bitcast.10, (f32[4,5,64]{2,1,0:T(8,128)}, f32[64,4,5,128]{3,0,2,1:T(8,128)S(1)}) %tuple.31, (s32[64]{0:T(128)S(1)}, s32[512]{0:T(512)S(1)}, bf16[1,128,2560]{2,1,0:T(8,128)(2,1)S(1)}, bf16[512,4,128]{0,2,1:T(8,128)(2,1)S(1)}, ...), branch_computations={%region_0.1_spmd, %region_1.4_spmd} | conditional | flops 344428288 | bytes 12239212 | solution.py:81
  48.8 0.0 copy-start.2
  48.8 0.7 broadcast_compare_fusion
  49.5 0.0 copy-done.2
  49.6 0.0 copy-start.3
  49.6 0.0 copy-start.4
  49.6 0.4 slice.17
  50.0 1.4 %fusion = (f32[4,5,64]{2,1,0:T(8,128)S(1)}, f32[4,512,64,5]{1,2,3,0:T(8,128)S(1)}) fusion(pred[64,512]{1,0:T(8,128)(4,1)} %broadcast_compare_fusion, bf16[64,4,5,128]{3,2,1,0:T(8,128)(2,1)S(1)} %slice.17, bf16[512,4,128]{0,2,1:T(8,128)(2,1)S(1)} %get-tuple-element.165), kind=kOutput, calls=%fused_computation.2 | convolution fusion | flops 169736960 | bytes 3511296 | tf_op jit(solution)/shard_map/while/body/eval_jaxpr/cond/branch_1_fun/rgqd,kgd->gqrk/dot_general | solution.py:26
  51.4 0.0 copy-done.3
  51.4 0.0 copy-done.4
  51.4 0.9 fusion.2
  52.3 1.3 multiply_add_fusion
  53.6 1.1 fusion.9
  54.7 0.0 copy-start.5
  54.7 1.0 divide_convert_fusion.1
  55.7 0.2 copy.27
  55.9 0.4 reshape.56
  56.3 0.0 copy-done.5
  56.3 0.1 fusion.59
  56.4 0.2 reduce_window_sum.11
  56.6 0.2 select_reduce_fusion
  56.8 0.2 convolution_convert_fusion
  57.0 6.4 %all_to_all.10 = bf16[2,2,2560]{2,1,0:T(2,128)(2,1)S(1)} all-to-all(bf16[2,2,2560]{2,1,0:T(2,128)(2,1)S(1)} %reshape.58), channel_id=1, replica_groups=mesh['groups'=2,'ctx'=4,'ep'=2,'tp'=2] {'ep'}, dimensions={0} | all-to-all | bytes 40960 | tf_op jit(solution)/shard_map/all_to_all | solution.py:113
  63.5 13.2 %all-gather = bf16[8,2,2560]{2,1,0:T(2,128)(2,1)S(1)} all-gather(bf16[2,2,2560]{2,1,0:T(2,128)(2,1)S(1)} %all_to_all.10), channel_id=2, replica_groups=mesh['groups'=2,'ctx'=4,'ep'=2,'tp'=2] {'ctx'}, dimensions={0}, use_global_device_ids=true | all-gather | bytes 102400 | tf_op jit(solution)/shard_map/all_gather | solution.py:120
  76.7 3.3 %fusion.51 = bf16[16,1024]{1,0:T(8,128)(2,1)S(1)} fusion(bf16[16,2560]{1,0:T(8,128)(2,1)S(1)} %reshape.59, bf16[1,2560,1024]{2,1,0:T(8,128)(2,1)} %param.17), kind=kOutput, calls=%fused_computation.51 | convolution fusion | flops 83902464 | bytes 5357568 | tf_op jit(solution)/shard_map/dot_general | solution.py:125
  80.0 0.0 copy-done
  80.0 0.1 fusion.58
  80.2 3.5 %all-reduce.1 = (bf16[16,1024]{1,0:T(8,128)(2,1)S(1)}, bf16[16,1]{0,1:T(2,128)(2,1)S(1)}) all-reduce(bf16[16,1024]{1,0:T(8,128)(2,1)S(1)} %fusion.51, bf16[16,1]{0,1:T(2,128)(2,1)S(1)} %fusion.58), channel_id=1, replica_groups=mesh['groups'=2,'ctx'=4,'ep'=2,'tp'=2] {'tp'}, use_global_device_ids=true, to_apply=%region_11.12 | all-reduce | flops 16400 | bytes 65600 | tf_op jit(solution)/shard_map/psum | solution.py:130
  83.6 3.3 %fusion.54 = bf16[16,1024]{1,0:T(8,128)(2,1)S(1)} fusion(bf16[16,2560]{1,0:T(8,128)(2,1)S(1)} %reshape.59, bf16[1,2560,1024]{2,1,0:T(8,128)(2,1)} %param.18), kind=kOutput, calls=%fused_computation.52 | convolution fusion | flops 83902464 | bytes 5357568 | tf_op jit(solution)/shard_map/dot_general | solution.py:126
  86.9 1.8 %all-gather.1 = bf16[32,1024]{1,0:T(8,128)(2,1)S(1)} all-gather(bf16[16,1024]{1,0:T(8,128)(2,1)S(1)} %fusion.54), channel_id=3, replica_groups=mesh['groups'=2,'ctx'=4,'ep'=2,'tp'=2] {'tp'}, dimensions={0}, use_global_device_ids=true | all-gather | bytes 98304 | tf_op jit(solution)/shard_map/all_gather | solution.py:128
  88.8 0.0 copy-start.6
  88.8 4.0 %fusion.48 = bf16[16,2560]{1,0:T(8,128)(2,1)} fusion(bf16[1,1024,2560]{2,1,0:T(8,128)(2,1)} %param.19, bf16[16,1024]{1,0:T(8,128)(2,1)S(1)} %reduce_sum.42, bf16[16,1024]{1,0:T(8,128)(2,1)S(1)} %get-tuple-element.178, f32[16]{0:T(128)S(1)} %divide_bitcast_fusion), kind=kOutput, calls=%fused_computation.49 | convolution fusion | flops 84090880 | bytes 5390400 | tf_op jit(solution)/shard_map/dot_general | solution.py:137
  92.8 0.0 all-reduce.4.cloned.1.call-update
  92.8 0.0 copy-done.6
  92.8 0.6 dynamic-slice
  94.0 31.6 %all-reduce.4.cloned.1.call-done = bf16[16,2560]{1,0:T(8,128)(2,1)} async-done(((bf16[16,2560]{1,0:T(8,128)(2,1)}), bf16[16,2560]{1,0:T(8,128)(2,1)}) %all-reduce.4.cloned.1.call-update) | async-done | bytes 81936
  125.7 0.8 constant_dynamic-slice_fusion
  126.5 6.4 %all_to_all.11 = bf16[2,2,2560]{2,1,0:T(2,128)(2,1)S(1)} all-to-all(bf16[2,2,2560]{2,1,0:T(2,128)(2,1)S(1)} %reshape.61), channel_id=1, replica_groups=mesh['groups'=2,'ctx'=4,'ep'=2,'tp'=2] {'ep'}, dimensions={0} | all-to-all | bytes 40960 | tf_op jit(solution)/shard_map/all_to_all | solution.py:142
  132.9 1.2 fusion.47
  (17 shorter events, 0.2 us)
Async XLA Ops:
  6.5 73.5 %copy-start = (bf16[2560,1]{0,1:T(2,128)(2,1)S(1)}, bf16[2560,1]{0,1:T(2,128)(2,1)}, u32[]{:S(2)}) copy-start(bf16[2560,1]{0,1:T(2,128)(2,1)} %param.16) | copy-start | bytes 15364
  6.5 119.2 %all-reduce.4.cloned.1.call-start = ((), (), s32[]{:S(2)}) async-start(), calls=%async_computation.2 | async-start | bytes 163840
  46.7 2.1 %copy-start.1 = (bf16[1,128,2560]{2,1,0:T(8,128)(2,1)S(1)}, bf16[1,128,2560]{2,1,0:T(8,128)(2,1)}, u32[]{:S(2)}) copy-start(bf16[1,128,2560]{2,1,0:T(8,128)(2,1)} %param.12) | copy-start | bytes 1966084
  48.8 0.7 copy-start.2
  49.6 1.8 %copy-start.3 = (f32[4,5,64]{2,1,0:T(8,128)S(1)}, f32[4,5,64]{2,1,0:T(8,128)}, u32[]{:S(2)}) copy-start(f32[4,5,64]{2,1,0:T(8,128)} %copy-done.2) | copy-start | bytes 15364 | tf_op jit(solution)/shard_map/while/body/eval_jaxpr/cond
  49.6 1.9 %copy-start.4 = (pred[64,512]{1,0:T(8,128)(4,1)S(1)}, pred[64,512]{1,0:T(8,128)(4,1)}, u32[]{:S(2)}) copy-start(pred[64,512]{1,0:T(8,128)(4,1)} %broadcast_compare_fusion) | copy-start | bytes 98308 | tf_op jit(solution)/shard_map/while/body/eval_jaxpr/cond
  54.7 1.6 %copy-start.5 = (s32[1,128,1]{1,2,0:T(1,128)S(1)}, s32[1,128,1]{1,2,0:T(1,128)}, u32[]{:S(2)}) copy-start(s32[1,128,1]{1,2,0:T(1,128)} %param.15) | copy-start | bytes 1540
  88.8 4.0 %copy-start.6 = (u32[32]{0:T(128)S(1)}, u32[32]{0:T(128)}, u32[]{:S(2)}) copy-start(u32[32]{0:T(128)} %constant.76) | copy-start | bytes 388
Sparse Core Ops, SparseCore 0:
  92.9 32.7 all-reduce.3
